TPU v7x, 32 devices: a whole 2x2x4 slice. The times are simulated.
32 devices in a mesh: dp: 16 (over z, x, core), stream: 2 (over y).
Axes of the slice: x: 2, y: 2, z: 4, core: 2. Of those that a mesh axis runs over, the one named last changes fastest.
Arguments:
- tokens: bfloat16 [80, 2, 200, 768], P('dp', 'stream'), may hold values from -6 to 6
- text_segment: int32 [80, 200], P('dp'), may hold values from 0 to 5, as said below
- ln1_gain: float32 [768], replicated, may hold values from 0.5 to 1.5
- ln1_bias: float32 [768], replicated, may hold values from -3 to 3
- qkv_weight: bfloat16 [768, 2304], replicated, may hold values from -0.3125 to 0.3125
- out_weight: bfloat16 [768, 768], replicated, may hold values from -0.625 to 0.625
- attn_scale: float32 [768], replicated, may hold values from 0.25 to 1.75
- ffn_scale: float32 [768], replicated, may hold values from 0.25 to 1.75
- ln2_gain: float32 [2, 768], P('stream'), may hold values from 0.5 to 1.5
- ln2_bias: float32 [2, 768], P('stream'), may hold values from -3 to 3
- expert_in: bfloat16 [2, 768, 3072], P('stream'), may hold values from -0.21875 to 0.21875
- expert_out: bfloat16 [2, 3072, 768], P('stream'), may hold values from -0.15625 to 0.15625
- out_cot: bfloat16 [80, 2, 200, 768], P('dp', 'stream'), may hold values from -6 to 6
Outputs:
- block_out: bfloat16 [80, 2, 200, 768], P('dp', 'stream')
- tokens_grad: bfloat16 [80, 2, 200, 768], P('dp', 'stream')
- ln1_gain_grad: float32 [768], replicated
- ln1_bias_grad: float32 [768], replicated
- qkv_weight_grad: float32 [768, 2304], replicated
- out_weight_grad: float32 [768, 768], replicated
- attn_scale_grad: float32 [768], replicated
- ffn_scale_grad: float32 [768], replicated
- ln2_gain_grad: float32 [2, 768], P('stream')
- ln2_bias_grad: float32 [2, 768], P('stream')
- expert_in_grad: float32 [2, 768, 3072], P('stream')
- expert_out_grad: float32 [2, 3072, 768], P('stream')
Inputs may be any that keep to these rules, and one draw needn't show every extreme that they name: `text_segment`: in each group the text slots hold the captions numbered below 5 in order, each of 1 to 39 slots, followed by padding slots numbered 5.
All inputs are finite; a program needn't handle non-finite values.
Results may differ from a plain program's by a relative error of at most 0.015.
The roundings to bfloat16 on the way count: a program that leaves them out, or rounds other values in their place, can miss the bound.
Values may be sent and summed in bfloat16 or wider, within the bound.
A program may use at most 256 MiB of HBM per device.

v0:
```python
import jax
import jax.numpy as jnp
from jax import lax
from jax.sharding import PartitionSpec as P

HEADS = 12
HDIM = 64
PATCHES = 197
CAPTIONS = 5
EPSILON = 1e-05


def layer_norm(inputs, gain_row, bias_row):
    row_mean = jnp.mean(inputs, axis=-1, keepdims=True)
    centered = inputs - row_mean
    variance = jnp.mean(centered * centered, axis=-1, keepdims=True)
    return centered * lax.rsqrt(variance + EPSILON) * gain_row + bias_row


def gelu_exact(inputs):
    return jax.nn.gelu(inputs, approximate=False)


def contract_rows(left_side, right_side):
    return lax.dot_general(
        left_side, right_side, (((0,), (0,)), ((), ())), preferred_element_type=jnp.float32
    )


def times_transposed(left_side, right_side):
    return lax.dot_general(
        left_side, right_side, (((1,), (1,)), ((), ())), preferred_element_type=jnp.float32
    )


def shards(
    tokens,
    text_segment,
    ln1_gain,
    ln1_bias,
    qkv_weight,
    out_weight,
    attn_scale,
    ffn_scale,
    ln2_gain,
    ln2_bias,
    expert_in,
    expert_out,
    out_cot,
):
    group_count = tokens.shape[0]
    slot_count = tokens.shape[2]
    model_width = tokens.shape[3]
    row_count = group_count * slot_count
    score_scale = HDIM ** (-0.5)
    stream_index = lax.axis_index("stream")
    flat_rows = tokens.reshape(row_count, model_width).astype(jnp.float32)
    attn_in, ln1_pull = jax.vjp(layer_norm, flat_rows, ln1_gain, ln1_bias)
    attn_low = attn_in.astype(jnp.bfloat16)
    qkv = jnp.dot(attn_low, qkv_weight, preferred_element_type=jnp.float32).astype(jnp.bfloat16)
    qkv_heads = qkv.reshape(group_count, slot_count, 3, HEADS, HDIM)
    queries = qkv_heads[:, :, 0]
    pairs = qkv_heads[:, :, 1:].reshape(group_count, 1, slot_count, 2 * model_width)
    gathered = lax.all_gather(pairs, "stream", axis=1, tiled=True)
    both_heads = gathered.reshape(group_count, 2 * slot_count, 2, HEADS, HDIM)
    key_all = both_heads[:, :, 0]
    value_all = both_heads[:, :, 1]
    slot_index = lax.broadcasted_iota(jnp.int32, (slot_count,), 0)
    patch_key = slot_index < PATCHES
    text_key = text_segment < CAPTIONS
    same_caption = text_segment[:, :, None] == text_segment[:, None, :]
    patch_part = jnp.broadcast_to(patch_key[None, None, :], (group_count, slot_count, slot_count))
    image_text = jnp.broadcast_to(text_key[:, None, :], (group_count, slot_count, slot_count))
    text_part = jnp.where(stream_index == 0, image_text, same_caption)
    visible = jnp.concatenate([patch_part, text_part], axis=2)[:, None]

    def masked_scores():
        scores = (
            jnp.einsum("gqhe,gkhe->ghqk", queries, key_all, preferred_element_type=jnp.float32)
            * score_scale
        )
        return jnp.where(visible, scores, jnp.float32(-1e30))

    scores = masked_scores()
    row_max = jnp.max(scores, axis=-1, keepdims=True)
    exp_terms = jnp.exp(scores - row_max)
    row_total = jnp.sum(exp_terms, axis=-1, keepdims=True)
    weights = exp_terms / row_total
    log_total = row_max + jnp.log(row_total)
    mixed_heads = jnp.einsum(
        "ghqk,gkhe->gqhe",
        weights.astype(jnp.bfloat16),
        value_all,
        preferred_element_type=jnp.float32,
    )
    mixed_heads = mixed_heads.astype(jnp.bfloat16).reshape(row_count, model_width)
    attn_proj = jnp.dot(mixed_heads, out_weight, preferred_element_type=jnp.float32)
    residual = flat_rows + attn_scale * attn_proj
    in_matrix = expert_in[0]
    out_matrix = expert_out[0]
    ffn_in, ln2_pull = jax.vjp(layer_norm, residual, ln2_gain[0], ln2_bias[0])
    ffn_low = ffn_in.astype(jnp.bfloat16)
    pre_act = jnp.dot(ffn_low, in_matrix, preferred_element_type=jnp.float32)
    activation = gelu_exact(pre_act).astype(jnp.bfloat16)
    ffn_out = jnp.dot(activation, out_matrix, preferred_element_type=jnp.float32)
    block_out = (residual + ffn_scale * ffn_out).astype(jnp.bfloat16)
    grad_out = out_cot.reshape(row_count, model_width).astype(jnp.float32)
    ffn_scale_grad = jnp.sum(grad_out * ffn_out, axis=0)
    grad_ffn = (ffn_scale * grad_out).astype(jnp.bfloat16)
    expert_out_grad = contract_rows(activation, grad_ffn)
    grad_act = times_transposed(grad_ffn, out_matrix)
    _, gelu_pull = jax.vjp(gelu_exact, pre_act)
    grad_pre = gelu_pull(grad_act)[0].astype(jnp.bfloat16)
    expert_in_grad = contract_rows(ffn_low, grad_pre)
    grad_ffn_in = times_transposed(grad_pre, in_matrix)
    grad_resid_norm, ln2_gain_grad, ln2_bias_grad = ln2_pull(grad_ffn_in)
    grad_resid = grad_out + grad_resid_norm
    expert_total = lax.psum((expert_in_grad, expert_out_grad, ln2_gain_grad, ln2_bias_grad), "dp")
    attn_scale_grad = jnp.sum(grad_resid * attn_proj, axis=0)
    grad_proj = (attn_scale * grad_resid).astype(jnp.bfloat16)
    out_weight_grad = contract_rows(mixed_heads, grad_proj)
    grad_mix = times_transposed(grad_proj, out_weight).astype(jnp.bfloat16)
    grad_mix = grad_mix.reshape(group_count, slot_count, HEADS, HDIM)
    weights_again = jnp.exp(masked_scores() - log_total)
    grad_probs = jnp.einsum(
        "gqhe,gkhe->ghqk", grad_mix, value_all, preferred_element_type=jnp.float32
    )
    inner_sum = jnp.sum(weights_again * grad_probs, axis=-1, keepdims=True)
    grad_scores = (weights_again * (grad_probs - inner_sum)).astype(jnp.bfloat16)
    grad_query = (
        jnp.einsum("ghqk,gkhe->gqhe", grad_scores, key_all, preferred_element_type=jnp.float32)
        * score_scale
    )
    grad_query = grad_query.astype(jnp.bfloat16).reshape(row_count, model_width)
    grad_key = (
        jnp.einsum("ghqk,gqhe->gkhe", grad_scores, queries, preferred_element_type=jnp.float32)
        * score_scale
    )
    grad_value = jnp.einsum(
        "ghqk,gqhe->gkhe",
        weights_again.astype(jnp.bfloat16),
        grad_mix,
        preferred_element_type=jnp.float32,
    )
    key_terms = jnp.stack([grad_key, grad_value], axis=2).reshape(
        group_count, 2, slot_count, 2 * model_width
    )
    owned_grads = lax.psum_scatter(
        key_terms.astype(jnp.bfloat16), "stream", scatter_dimension=1, tiled=True
    ).astype(jnp.float32)
    owned_grads = owned_grads.reshape(row_count, 2 * model_width).astype(jnp.bfloat16)
    grad_qkv = jnp.concatenate([grad_query, owned_grads], axis=1)
    qkv_weight_grad = contract_rows(attn_low, grad_qkv)
    grad_attn_in = times_transposed(grad_qkv, qkv_weight)
    grad_rows_norm, ln1_gain_grad, ln1_bias_grad = ln1_pull(grad_attn_in)
    tokens_grad = (grad_resid + grad_rows_norm).astype(jnp.bfloat16).reshape(tokens.shape)
    small_grads = jnp.stack([ln1_gain_grad, ln1_bias_grad, attn_scale_grad, ffn_scale_grad], axis=0)
    shared_total = lax.psum((qkv_weight_grad, out_weight_grad, small_grads), ("dp", "stream"))
    small_total = shared_total[2]
    return (
        block_out.reshape(tokens.shape),
        tokens_grad,
        small_total[0],
        small_total[1],
        shared_total[0],
        shared_total[1],
        small_total[2],
        small_total[3],
        expert_total[2][None, :],
        expert_total[3][None, :],
        expert_total[0][None, :, :],
        expert_total[1][None, :, :],
    )


def solution(mesh):
    placed = (
        P("dp", "stream", None, None),
        P("dp", None),
        P(),
        P(),
        P(),
        P(),
        P(),
        P(),
        P("stream", None),
        P("stream", None),
        P("stream", None, None),
        P("stream", None, None),
        P("dp", "stream", None, None),
    )
    return jax.shard_map(
        shards,
        mesh=mesh,
        in_specs=placed,
        out_specs=(
            P("dp", "stream", None, None),
            P("dp", "stream", None, None),
            P(),
            P(),
            P(),
            P(),
            P(),
            P(),
            P("stream", None),
            P("stream", None),
            P("stream", None, None),
            P("stream", None, None),
        ),
        check_vma=False,
    )
```

profile of v0, /device:TPU:0, one launch (start us, length us, event | category | flops | bytes accessed | tf_op | source)
XLA Modules:
  0.0 1063.4 jit_solution(14414983165366514719)
XLA Ops:
  29.6 15.1 %reshape.175 = bf16[5,200,3,12,64]{1,0,4,3,2:T(8,128)(2,1)} reshape(bf16[1000,2304]{0,1:T(8,128)(2,1)} %copy.61) | data formatting | bytes 9216000 | tf_op jit(solution)/shard_map/reshape | solution.py:61
  66.8 72.7 %all-gather.2.cloned.1.call-done = bf16[5,2,200,1536]{3,2,0,1:T(8,128)(2,1)} async-done(((bf16[5,1,200,1536]{3,2,0,1:T(8,128)(2,1)}), bf16[5,2,200,1536]{3,2,0,1:T(8,128)(2,1)}) %all-gather.2.cloned.1.call-update) | async-done | bytes 6144016 | tf_op jit(solution)/shard_map/all_gather | solution.py:64
  139.5 20.1 %copy.64 = bf16[5,2,200,1536]{2,1,3,0:T(2,128)(2,1)} copy(bf16[5,2,200,1536]{3,2,0,1:T(8,128)(2,1)} %all-gather.2.cloned.1.call-done) | data formatting | bytes 12288000 | tf_op jit(solution)/shard_map/all_gather | solution.py:64
  159.6 13.1 %reshape.177 = bf16[5,400,2,12,64]{1,4,3,2,0:T(8,128)(2,1)} reshape(bf16[5,2,200,1536]{2,1,3,0:T(2,128)(2,1)} %copy.64) | data formatting | bytes 12288000 | tf_op jit(solution)/shard_map/reshape | solution.py:65
  172.7 15.1 %fusion.39 = (f32[5,12,200]{2,1,0:T(8,128)S(1)}, f32[5,12,200,400]{3,2,1,0:T(8,128)}) fusion(bf16[5,400,2,12,64]{1,4,3,2,0:T(8,128)(2,1)} %reshape.177, bf16[5,200,1,12,64]{1,0,4,3,2:T(8,128)(2,1)} %slice.34, pred[5,200,400]{2,1,0:T(8,128)(4,1)} %pad_add_fusion), kind=kOutput, calls=%fused_computation.101 | convolution fusion | flops 628787968 | bytes 26837888 | tf_op jit(solution)/shard_map/gqhe,gkhe->ghqk/dot_general | solution.py:79
  187.9 11.5 %fusion = f32[5,12,200]{2,1,0:T(8,128)S(1)} fusion(f32[5,12,200,400]{3,2,1,0:T(8,128)} %get-tuple-element.88, f32[5,12,200]{2,1,0:T(8,128)S(1)} %get-tuple-element.87), kind=kLoop, calls=%fused_computation.6 | loop fusion | flops 9588000 | bytes 19296000 | tf_op jit(solution)/shard_map/reduce_sum | solution.py:87
  199.4 11.2 %convert_bitcast_fusion.1 = bf16[5,200,12,64]{1,3,2,0:T(8,128)(2,1)S(1)} fusion(f32[5,12,200,400]{3,2,1,0:T(8,128)} %get-tuple-element.88, f32[5,12,200]{2,1,0:T(8,128)S(1)} %fusion, f32[5,12,200]{2,1,0:T(8,128)S(1)} %get-tuple-element.87, bf16[5,400,2,12,64]{1,4,3,2,0:T(8,128)(2,1)S(1)} %copy-done.3), kind=kOutput, calls=%fused_computation.76 | convolution fusion | flops 629568000 | bytes 24832000 | tf_op jit(solution)/shard_map/ghqk,gkhe->gqhe/dot_general | solution.py:90
  230.7 35.5 %multiply_convert_fusion.1 = (bf16[1000,3072]{1,0:T(8,128)(2,1)}, f32[1000,3072]{1,0:T(8,128)}, f32[1000,3072]{1,0:T(8,128)}) fusion(bf16[1,768,3072]{2,1,0:T(8,128)(2,1)} %param.23, f32[1000,768]{1,0:T(8,128)} %get-tuple-element.89, f32[768]{0:T(1024)S(1)} %reduce.5, f32[768]{0:T(1024)S(1)} %reduce.4, f32[1000]{0:T(1024)S(1)} %fusion.34, ...), kind=kOutput, calls=%fused_computation.13 | convolution fusion | flops 4922112000 | bytes 38524736 | tf_op jit(solution)/shard_map/dot_general | solution.py:103
  266.2 15.5 %add_convert_fusion = bf16[1000,3072]{1,0:T(8,128)(2,1)} fusion(f32[1000,3072]{1,0:T(8,128)} %get-tuple-element.81, f32[1000,3072]{1,0:T(8,128)} %get-tuple-element.91, bf16[1000,768]{1,0:T(8,128)(2,1)S(1)} %bitcast.116, bf16[1,3072,768]{2,1,0:T(8,128)(2,1)} %param.24), kind=kOutput, calls=%fused_computation.12 | convolution fusion | flops 4761600000 | bytes 36974592 | tf_op jit(solution)/shard_map/dot_general | solution.py:31
  281.8 10.3 multiply_reduce_fusion.1
  292.1 10.7 %fusion.26 = (f32[768]{0:T(1024)}, bf16[1000,768]{1,0:T(8,128)(2,1)}, f32[1000]{0:T(1024)S(1)}, f32[1000,768]{1,0:T(8,128)S(1)}, bf16[1000,768]{1,0:T(8,128)(2,1)}) fusion(bf16[5,1,200,768]{3,2,1,0:T(8,128)(2,1)S(1)} %copy-done.9, f32[1000,768]{1,0:T(8,128)S(1)} %copy-done.2, f32[768]{0:T(1024)S(1)} %copy-done.27, f32[1000]{0:T(1024)S(1)} %multiply_multiply_fusion.6, ...), kind=kOutput, calls=%fused_computation.56 | convolution fusion | flops 4730109952 | bytes 24711808 | tf_op jit(solution)/shard_map/dot_general | solution.py:105
  320.0 22.1 %multiply_reduce_fusion = (f32[5,12,200]{2,1,0:T(8,128)S(1)}, f32[5,12,200,400]{3,2,1,0:T(8,128)}) fusion(f32[5,12,200,400]{3,2,1,0:T(8,128)} %get-tuple-element.88, f32[5,12,200]{2,1,0:T(8,128)} %log_add_fusion, bf16[5,200,12,64]{1,3,2,0:T(8,128)(2,1)} %copy.70, bf16[5,400,2,12,64]{1,4,3,2,0:T(8,128)(2,1)} %reshape.177), kind=kOutput, calls=%fused_computation.1 | convolution fusion | flops 628787968 | bytes 49804160 | tf_op jit(solution)/shard_map/gqhe,gkhe->ghqk/dot_general | solution.py:125
  342.1 12.6 %convert_bitcast_fusion = bf16[5,400,1,12,64]{1,4,3,0,2:T(8,128)(2,1)} fusion(bf16[5,200,12,64]{1,3,2,0:T(8,128)(2,1)S(1)} %copy-done.6, f32[5,12,200,400]{3,2,1,0:T(8,128)} %get-tuple-element.88, f32[5,12,200]{2,1,0:T(8,128)S(1)} %copy-done.11), kind=kOutput, calls=%fused_computation.47 | convolution fusion | flops 625536000 | bytes 23856000 | tf_op jit(solution)/shard_map/ghqk,gqhe->gkhe/dot_general | solution.py:139
  354.7 16.3 %multiply_convert_fusion = bf16[5,12,200,400]{3,2,1,0:T(8,128)(2,1)S(1)} fusion(f32[5,12,200,400]{3,2,1,0:T(8,128)} %get-tuple-element.94, f32[5,12,200,400]{3,2,1,0:T(8,128)} %get-tuple-element.88, f32[5,12,200]{2,1,0:T(8,128)S(1)} %get-tuple-element.93, f32[5,12,200]{2,1,0:T(8,128)S(1)} %copy-done.11), kind=kLoop, calls=%fused_computation | loop fusion | flops 19200000 | bytes 48096000 | tf_op jit(solution)/shard_map/convert_element_type | solution.py:129
  394.3 13.2 %convert_element_type.107 = bf16[5,2,200,1536]{2,1,3,0:T(2,128)(2,1)} reshape(bf16[5,400,2,12,64]{1,4,3,2,0:T(8,128)(2,1)} %copy.73) | data formatting | bytes 12288000 | tf_op jit(solution)/shard_map/convert_element_type | solution.py:149
  407.4 19.6 %copy.74 = bf16[5,2,200,1536]{3,2,0,1:T(8,128)(2,1)} copy(bf16[5,2,200,1536]{2,1,3,0:T(2,128)(2,1)} %convert_element_type.107) | data formatting | bytes 12288000 | tf_op jit(solution)/shard_map/convert_element_type | solution.py:149
  427.1 11.2 %convolution_bitcast_fusion.1 = f32[1,768,3072]{2,1,0:T(8,128)} fusion(bf16[1000,3072]{1,0:T(8,128)(2,1)} %add_convert_fusion, f32[1000,768]{1,0:T(8,128)} %get-tuple-element.89, f32[768]{0:T(1024)S(1)} %reduce.5, f32[768]{0:T(1024)S(1)} %reduce.4, f32[1000]{0:T(1024)S(1)} %fusion.34, f32[1000]{0:T(1024)S(1)} %broadcast_multiply_fusion.1), kind=kOutput, calls=%fused_computation.31 | convolution fusion | flops 4722432000 | bytes 18667328 | tf_op jit(solution)/shard_map/dot_general | solution.py:25
  438.3 10.4 convolution_bitcast_fusion
  448.9 11.3 %fusion.32 = bf16[5,200,12,64]{1,3,2,0:T(8,128)(2,1)} fusion(bf16[5,12,200,400]{3,2,1,0:T(8,128)(2,1)} %copy-done.1, bf16[5,400,2,12,64]{1,4,3,2,0:T(8,128)(2,1)} %reshape.177), kind=kOutput, calls=%fused_computation.74 | convolution fusion | flops 615936000 | bytes 17756160 | tf_op jit(solution)/shard_map/ghqk,gkhe->gqhe/dot_general | solution.py:131
  477.8 25.0 %reduce-scatter.2.cloned.1.call-done = bf16[5,1,200,1536]{3,2,0,1:T(8,128)(2,1)} async-done(((bf16[5,2,200,1536]{3,2,0,1:T(8,128)(2,1)}), bf16[5,1,200,1536]{3,2,0,1:T(8,128)(2,1)}) %reduce-scatter.2.cloned.1.call-update) | async-done | bytes 3072016 | tf_op jit(solution)/shard_map/reduce_scatter | solution.py:148
  516.9 36.8 %all-reduce.1 = (f32[1,768]{1,0:T(1,128)}, f32[1,768]{1,0:T(1,128)}) all-reduce(f32[1,768]{1,0:T(1,128)} %broadcast_in_dim.76, f32[1,768]{1,0:T(1,128)} %broadcast_in_dim.77), channel_id=1, replica_groups=mesh['dp'=16,'stream'=2] {'dp'}, use_global_device_ids=true, to_apply=%region_20.21 | all-reduce | flops 1536 | bytes 12288 | tf_op jit(solution)/shard_map/psum | solution.py:118
  568.7 38.9 %psum.49 = f32[4,768]{1,0:T(4,128)S(1)} all-reduce(f32[4,768]{1,0:T(4,128)} %pad_maximum_fusion.4), channel_id=1, replica_groups=mesh['dp'=16,'stream'=2] {'dp','stream'}, use_global_device_ids=true, to_apply=%region_16.17 | all-reduce | flops 3072 | bytes 24576 | tf_op jit(solution)/shard_map/psum | solution.py:158
  612.5 225.5 %all-reduce.8.cloned.1.call-done = (f32[1,768,3072]{2,1,0:T(8,128)}, f32[1,3072,768]{2,1,0:T(8,128)}) async-done(((f32[1,768,3072]{2,1,0:T(8,128)}, f32[1,3072,768]{2,1,0:T(8,128)}), (f32[1,768,3072]{2,1,0:T(8,128)}, f32[1,3072,768]{2,1,0:T(8,128)})) %all-reduce.8.cloned.1.call-update) | async-done | bytes 18874384 | tf_op jit(solution)/shard_map/psum | solution.py:118
  838.0 197.6 %all-reduce.6.cloned.1.call-done = (f32[768,2304]{1,0:T(8,128)}, f32[768,768]{1,0:T(8,128)}) async-done(((f32[768,2304]{1,0:T(8,128)}, f32[768,768]{1,0:T(8,128)}), (f32[768,2304]{1,0:T(8,128)}, f32[768,768]{1,0:T(8,128)})) %all-reduce.6.cloned.1.call-update) | async-done | bytes 9437200 | tf_op jit(solution)/shard_map/psum | solution.py:158
  (137 shorter events, 178.0 us)
Async XLA Ops:
  7.2 10.5 copy-start
  7.2 132.3 %all-gather.2.cloned.1.call-start = ((), (), s32[]{:S(2)}) async-start(), calls=%async_computation.1 | async-start | bytes 9216000 | tf_op jit(solution)/shard_map/all_gather | solution.py:64
  11.7 11.3 %copy-start.16 = (f32[1000]{0:T(1024)}, f32[1000]{0:T(1024)S(1)}, u32[]{:S(2)}) copy-start(f32[1000]{0:T(1024)S(1)} %div.47) | copy-start | bytes 12004
  13.8 9.2 copy-start.20
  58.0 444.8 %reduce-scatter.2.cloned.1.call-start = ((), (), s32[]{:S(2)}) async-start(), calls=%async_computation.2 | async-start | bytes 9216000 | tf_op jit(solution)/shard_map/reduce_scatter | solution.py:148
  187.9 11.5 %copy-start.3 = (bf16[5,400,2,12,64]{1,4,3,2,0:T(8,128)(2,1)S(1)}, bf16[5,400,2,12,64]{1,4,3,2,0:T(8,128)(2,1)}, u32[]{:S(2)}) copy-start(bf16[5,400,2,12,64]{1,4,3,2,0:T(8,128)(2,1)} %reshape.177) | copy-start | bytes 18432004
  230.7 35.5 %copy-start.13 = (bf16[5,1,200,768]{3,2,1,0:T(8,128)(2,1)S(1)}, bf16[5,1,200,768]{3,2,1,0:T(8,128)(2,1)}, u32[]{:S(2)}) copy-start(bf16[5,1,200,768]{3,2,1,0:T(8,128)(2,1)} %fusion.25) | copy-start | bytes 4608004
  266.2 15.5 %copy-start.2 = (f32[1000,768]{1,0:T(8,128)S(1)}, f32[1000,768]{1,0:T(8,128)}, u32[]{:S(2)}) copy-start(f32[1000,768]{1,0:T(8,128)} %get-tuple-element.89) | copy-start | bytes 9216004
  281.7 10.3 copy-start.9
  281.7 10.3 copy-start.27
  281.7 10.3 copy-start.29
  292.1 10.7 %copy-start.5 = (f32[1000,768]{1,0:T(8,128)S(1)}, f32[1000,768]{1,0:T(8,128)}, u32[]{:S(2)}) copy-start(f32[1000,768]{1,0:T(8,128)} %get-tuple-element.90) | copy-start | bytes 9216004
  320.0 22.1 %copy-start.6 = (bf16[5,200,12,64]{1,3,2,0:T(8,128)(2,1)S(1)}, bf16[5,200,12,64]{1,3,2,0:T(8,128)(2,1)}, u32[]{:S(2)}) copy-start(bf16[5,200,12,64]{1,3,2,0:T(8,128)(2,1)} %copy.70) | copy-start | bytes 4608004
  320.0 22.1 %copy-start.11 = (f32[5,12,200]{2,1,0:T(8,128)S(1)}, f32[5,12,200]{2,1,0:T(8,128)}, u32[]{:S(2)}) copy-start(f32[5,12,200]{2,1,0:T(8,128)} %log_add_fusion) | copy-start | bytes 144004
  354.7 20.8 %copy-start.7 = (bf16[5,200,1,12,64]{1,0,4,3,2:T(8,128)(2,1)S(1)}, bf16[5,200,1,12,64]{1,0,4,3,2:T(8,128)(2,1)}, u32[]{:S(2)}) copy-start(bf16[5,200,1,12,64]{1,0,4,3,2:T(8,128)(2,1)} %slice.34) | copy-start | bytes 4608004
  427.0 411.0 %all-reduce.8.cloned.1.call-start = ((), (), s32[]{:S(2)}) async-start(), calls=%async_computation.4 | async-start | bytes 37748736 | tf_op jit(solution)/shard_map/psum | solution.py:118
  427.1 11.2 %copy-start.30 = (bf16[1000,768]{1,0:T(8,128)(2,1)S(1)}, bf16[1000,768]{1,0:T(8,128)(2,1)}, u32[]{:S(2)}) copy-start(bf16[1000,768]{1,0:T(8,128)(2,1)} %get-tuple-element.86) | copy-start | bytes 4608004
  448.7 586.9 %all-reduce.6.cloned.1.call-start = ((), (), s32[]{:S(2)}) async-start(), calls=%async_computation.3 | async-start | bytes 18874368 | tf_op jit(solution)/shard_map/psum | solution.py:158
  512.4 41.3 %copy-start.17 = (f32[1000]{0:T(1024)S(1)}, f32[1000]{0:T(1024)}, u32[]{:S(2)}) copy-start(f32[1000]{0:T(1024)} %copy-done.16) | copy-start | bytes 12004
  512.4 41.3 %copy-start.19 = (f32[1000]{0:T(1024)S(1)}, f32[1000]{0:T(1024)}, u32[]{:S(2)}) copy-start(f32[1000]{0:T(1024)} %copy-done.18) | copy-start | bytes 12004
  512.4 41.3 %copy-start.25 = (f32[768]{0:T(1024)S(1)}, f32[768]{0:T(1024)}, u32[]{:S(2)}) copy-start(f32[768]{0:T(1024)} %param.15) | copy-start | bytes 9220
  1042.2 10.7 %slice-start = ((s8[9437184]{0:T(1024)(128)(4,1)}), s8[4194304]{0:T(1024)(128)(4,1)S(1)}, s32[]{:S(2)}) async-start(s8[9437184]{0:T(1024)(128)(4,1)} %bitcast.114), calls=%async_computation.5 | async-start | bytes 8388608
  1043.6 9.3 slice-start.1
  1043.6 9.3 slice-start.2
  (14 other events, 64.1 us)
Sparse Core Ops, SparseCore 0:
  58.1 81.4 all-gather.1
  427.2 75.5 reduce-scatter.1
  507.4 330.5 all-reduce.7
  844.4 191.1 all-reduce.5
where the time goes:
time: 1070 us; the launch traced here: 1060 us
  waiting for transfers between devices  521 us (49%)
  matrix products  207 us (19%)
  local copies, waits for them, and re-layouts  181 us (17%)
  blocking collectives  75.6 us (7%)
  other arithmetic  64.7 us (6%)
  between operations  14.3 us (1%)
    psum x1, waiting for transfers between devices, shards(): lax.psum((expert_in_grad, expert_out_grad, ln2_gain_grad, ln2_bias_grad),...  226 us
    psum x1, waiting for transfers between devices, shards(): lax.psum((qkv_weight_grad, out_weight_grad, small_grads), ('dp', 'stream'))  198 us
    all_gather x1, waiting for transfers between devices, shards(): gathered = lax.all_gather(pairs, 'stream', axis=1, tiled=True)  72.7 us
    psum x1, blocking collectives, shards(): lax.psum((qkv_weight_grad, out_weight_grad, small_grads), ('dp', 'stream'))  38.9 us
    psum x1, blocking collectives, shards(): lax.psum((expert_in_grad, expert_out_grad, ln2_gain_grad, ln2_bias_grad),...  36.8 us
    dot_general x4, matrix products, contract_rows(): lax.dot_general(left_side, right_side, (((0,), (0,)), ((), ())), preferre...  36.4 us
    dot_general x4, matrix products, times_transposed(): lax.dot_general(left_side, right_side, (((1,), (1,)), ((), ())), preferre...  36.2 us
    dot_general x1, matrix products, shards(): pre_act = jnp.dot(ffn_low, in_matrix, preferred_element_type=jnp.float32)  35.5 us
  transfers between devices with their start and end apart: 4, of which 4 were waited for; matrix products, arithmetic and copies ran while one was open for 9% of the time, Pallas kernels for 0%

commit v1 on v0

--- a/solution.py
+++ b/solution.py
@@ -61,7 +61,9 @@
     qkv_heads = qkv.reshape(group_count, slot_count, 3, HEADS, HDIM)
     queries = qkv_heads[:, :, 0]
     pairs = qkv_heads[:, :, 1:].reshape(group_count, 1, slot_count, 2 * model_width)
-    gathered = lax.all_gather(pairs, "stream", axis=1, tiled=True)
+    gathered = jnp.concatenate(
+        lax.all_to_all(jnp.stack([pairs] * lax.axis_size("stream")), "stream", 0, 0), axis=1
+    )
     both_heads = gathered.reshape(group_count, 2 * slot_count, 2, HEADS, HDIM)
     key_all = both_heads[:, :, 0]
     value_all = both_heads[:, :, 1]

time: 1070 us -> 1010 us (0.944)
  waiting for transfers between devices: 521 us -> 449 us
    all_gather x1 -> x0, waiting for transfers between devices: 72.7 us -> none  [shards(): gathered = lax.all_gather(pairs, 'stream', axis=1, tiled=True)]
    all_to_all x0 -> x1, waiting for transfers between devices: none -> 61 us  [shards(): lax.all_to_all(jnp.stack([pairs] * lax.axis_size('stream')), 'stream', 0, 0)]
    psum x1, waiting for transfers between devices: 226 us -> 165 us  [shards(): lax.psum((expert_in_grad, expert_out_grad, ln2_gain_grad, ln2_bias_grad),...]
    another operation x0 -> x2, local copies, waits for them, and re-layouts: none -> 22.8 us  [the longest x1 13.1 us: shards(): both_heads = gathered.reshape(group_count, 2 * slot_count, 2, HEADS, HDIM)]
    all_gather x1 -> x0, local copies, waits for them, and re-layouts: 20.1 us -> none  [shards(): gathered = lax.all_gather(pairs, 'stream', axis=1, tiled=True)]
where the time goes in v1:
time: 1010 us; the launch traced here: 1000 us
  waiting for transfers between devices  449 us (44%)
  matrix products  207 us (20%)
  local copies, waits for them, and re-layouts  181 us (18%)
  blocking collectives  75.7 us (7%)
  other arithmetic  69.5 us (7%)
  between operations  16.1 us (2%)
    psum x1, waiting for transfers between devices, shards(): lax.psum((qkv_weight_grad, out_weight_grad, small_grads), ('dp', 'stream'))  197 us
    psum x1, waiting for transfers between devices, shards(): lax.psum((expert_in_grad, expert_out_grad, ln2_gain_grad, ln2_bias_grad),...  165 us
    all_to_all x1, waiting for transfers between devices, shards(): lax.all_to_all(jnp.stack([pairs] * lax.axis_size('stream')), 'stream', 0, 0)  61 us
    psum x1, blocking collectives, shards(): lax.psum((qkv_weight_grad, out_weight_grad, small_grads), ('dp', 'stream'))  38.9 us
    psum x1, blocking collectives, shards(): lax.psum((expert_in_grad, expert_out_grad, ln2_gain_grad, ln2_bias_grad),...  36.7 us
    dot_general x4, matrix products, contract_rows(): lax.dot_general(left_side, right_side, (((0,), (0,)), ((), ())), preferre...  36.5 us
    dot_general x4, matrix products, times_transposed(): lax.dot_general(left_side, right_side, (((1,), (1,)), ((), ())), preferre...  36.2 us
    dot_general x1, matrix products, shards(): pre_act = jnp.dot(ffn_low, in_matrix, preferred_element_type=jnp.float32)  35.5 us
  transfers between devices with their start and end apart: 4, of which 4 were waited for; matrix products, arithmetic and copies ran while one was open for 9% of the time, Pallas kernels for 0%

profile of v1, /device:TPU:0, one launch (start us, length us, event | category | flops | bytes accessed | tf_op | source)
XLA Modules:
  0.0 1004.6 jit_solution(10668912749533286006)
XLA Ops:
  30.4 15.1 %reshape.172 = bf16[5,200,3,12,64]{1,0,4,3,2:T(8,128)(2,1)} reshape(bf16[1000,2304]{0,1:T(8,128)(2,1)} %copy.61) | data formatting | bytes 9216000 | tf_op jit(solution)/shard_map/reshape | solution.py:61
  78.8 61.0 %all-to-all-done = bf16[2,5,1,200,1536]{4,3,2,1,0:T(8,128)(2,1)} async-done(((bf16[2,5,1,200,1536]{4,3,2,1,0:T(8,128)(2,1)}), bf16[2,5,1,200,1536]{4,3,2,1,0:T(8,128)(2,1)}, u32[]{:S(2)}, u32[]{:S(2)}) %all-to-all-start) | async-done | bytes 6144032 | tf_op jit(solution)/shard_map/all_to_all | solution.py:65
  139.8 20.1 %copy.64 = bf16[5,2,1,200,1536]{3,1,4,0,2:T(2,128)(2,1)} copy(bf16[5,2,1,200,1536]{4,3,2,0,1:T(8,128)(2,1)} %bitcast.2) | data formatting | bytes 12288000 | tf_op jit(solution)/shard_map/reshape | solution.py:64
  159.9 13.1 %reshape_reshape.3 = bf16[5,400,2,12,64]{1,4,3,2,0:T(8,128)(2,1)} reshape(bf16[5,2,1,200,1536]{3,1,4,0,2:T(2,128)(2,1)} %copy.64) | data formatting | bytes 12288000 | tf_op jit(solution)/shard_map/reshape;reshape | solution.py:67
  173.0 15.1 %fusion.39 = (f32[5,12,200]{2,1,0:T(8,128)S(1)}, f32[5,12,200,400]{3,2,1,0:T(8,128)}) fusion(bf16[5,400,2,12,64]{1,4,3,2,0:T(8,128)(2,1)} %reshape_reshape.3, bf16[5,200,1,12,64]{1,0,4,3,2:T(8,128)(2,1)} %slice.34, pred[5,200,400]{2,1,0:T(8,128)(4,1)} %pad_add_fusion), kind=kOutput, calls=%fused_computation.102 | convolution fusion | flops 628787968 | bytes 26837888 | tf_op jit(solution)/shard_map/gqhe,gkhe->ghqk/dot_general | solution.py:81
  188.1 11.5 %fusion = f32[5,12,200]{2,1,0:T(8,128)S(1)} fusion(f32[5,12,200,400]{3,2,1,0:T(8,128)} %get-tuple-element.88, f32[5,12,200]{2,1,0:T(8,128)S(1)} %get-tuple-element.87), kind=kLoop, calls=%fused_computation.6 | loop fusion | flops 9588000 | bytes 19296000 | tf_op jit(solution)/shard_map/reduce_sum | solution.py:89
  199.7 11.2 %convert_bitcast_fusion.1 = bf16[5,200,12,64]{1,3,2,0:T(8,128)(2,1)S(1)} fusion(f32[5,12,200,400]{3,2,1,0:T(8,128)} %get-tuple-element.88, f32[5,12,200]{2,1,0:T(8,128)S(1)} %fusion, f32[5,12,200]{2,1,0:T(8,128)S(1)} %get-tuple-element.87, bf16[5,400,2,12,64]{1,4,3,2,0:T(8,128)(2,1)S(1)} %copy-done.3), kind=kOutput, calls=%fused_computation.77 | convolution fusion | flops 629568000 | bytes 24832000 | tf_op jit(solution)/shard_map/ghqk,gkhe->gqhe/dot_general | solution.py:92
  231.0 35.5 %multiply_convert_fusion.1 = (bf16[1000,3072]{1,0:T(8,128)(2,1)}, f32[1000,3072]{1,0:T(8,128)}, f32[1000,3072]{1,0:T(8,128)}) fusion(bf16[1,768,3072]{2,1,0:T(8,128)(2,1)} %param.23, f32[1000,768]{1,0:T(8,128)} %get-tuple-element.89, f32[768]{0:T(1024)S(1)} %reduce.5, f32[768]{0:T(1024)S(1)} %reduce.4, f32[1000]{0:T(1024)S(1)} %fusion.34, ...), kind=kOutput, calls=%fused_computation.13 | convolution fusion | flops 4922112000 | bytes 38524736 | tf_op jit(solution)/shard_map/dot_general | solution.py:105
  266.5 15.5 %add_convert_fusion = bf16[1000,3072]{1,0:T(8,128)(2,1)} fusion(f32[1000,3072]{1,0:T(8,128)} %get-tuple-element.81, f32[1000,3072]{1,0:T(8,128)} %get-tuple-element.91, bf16[1000,768]{1,0:T(8,128)(2,1)S(1)} %bitcast.117, bf16[1,3072,768]{2,1,0:T(8,128)(2,1)} %param.24), kind=kOutput, calls=%fused_computation.12 | convolution fusion | flops 4761600000 | bytes 36974592 | tf_op jit(solution)/shard_map/dot_general | solution.py:31
  282.0 10.3 %multiply_reduce_fusion.1 = (f32[768]{0:T(1024)}, f32[1000]{0:T(1024)S(1)}, f32[768]{0:T(1024)}, f32[1000,768]{1,0:T(8,128)S(1)}) fusion(f32[1000,768]{1,0:T(8,128)S(1)} %copy-done.2, f32[1000]{0:T(1024)S(1)} %fusion.34, f32[1000]{0:T(1024)S(1)} %broadcast_multiply_fusion.1, f32[768]{0:T(1024)S(1)} %reduce.4, bf16[1000,3072]{1,0:T(8,128)(2,1)} %add_convert_fusion, ...), kind=kOutput, calls=%fused_computation.59 | convolution fusion | flops 4724732928 | bytes 17027808 | tf_op jit(solution)/shard_map/dot_general | solution.py:31
  292.4 10.7 %fusion.26 = (f32[768]{0:T(1024)}, bf16[1000,768]{1,0:T(8,128)(2,1)}, f32[1000]{0:T(1024)S(1)}, f32[1000,768]{1,0:T(8,128)S(1)}, bf16[1000,768]{1,0:T(8,128)(2,1)}) fusion(bf16[5,1,200,768]{3,2,1,0:T(8,128)(2,1)S(1)} %copy-done.9, f32[1000,768]{1,0:T(8,128)S(1)} %copy-done.2, f32[768]{0:T(1024)S(1)} %copy-done.27, f32[1000]{0:T(1024)S(1)} %multiply_multiply_fusion.6, ...), kind=kOutput, calls=%fused_computation.57 | convolution fusion | flops 4730109952 | bytes 24711808 | tf_op jit(solution)/shard_map/dot_general | solution.py:107
  320.3 22.1 %multiply_reduce_fusion = (f32[5,12,200]{2,1,0:T(8,128)S(1)}, f32[5,12,200,400]{3,2,1,0:T(8,128)}) fusion(f32[5,12,200,400]{3,2,1,0:T(8,128)} %get-tuple-element.88, f32[5,12,200]{2,1,0:T(8,128)} %log_add_fusion, bf16[5,200,12,64]{1,3,2,0:T(8,128)(2,1)} %copy.70, bf16[5,400,2,12,64]{1,4,3,2,0:T(8,128)(2,1)} %reshape_reshape.3), kind=kOutput, calls=%fused_computation.1 | convolution fusion | flops 628787968 | bytes 49804160 | tf_op jit(solution)/shard_map/gqhe,gkhe->ghqk/dot_general | solution.py:127
  342.4 12.6 %convert_bitcast_fusion = bf16[5,400,1,12,64]{1,4,3,0,2:T(8,128)(2,1)} fusion(bf16[5,200,12,64]{1,3,2,0:T(8,128)(2,1)S(1)} %copy-done.6, f32[5,12,200,400]{3,2,1,0:T(8,128)} %get-tuple-element.88, f32[5,12,200]{2,1,0:T(8,128)S(1)} %copy-done.11), kind=kOutput, calls=%fused_computation.48 | convolution fusion | flops 625536000 | bytes 23856000 | tf_op jit(solution)/shard_map/ghqk,gqhe->gkhe/dot_general | solution.py:141
  355.0 16.3 %multiply_convert_fusion = bf16[5,12,200,400]{3,2,1,0:T(8,128)(2,1)S(1)} fusion(f32[5,12,200,400]{3,2,1,0:T(8,128)} %get-tuple-element.94, f32[5,12,200,400]{3,2,1,0:T(8,128)} %get-tuple-element.88, f32[5,12,200]{2,1,0:T(8,128)S(1)} %get-tuple-element.93, f32[5,12,200]{2,1,0:T(8,128)S(1)} %copy-done.11), kind=kLoop, calls=%fused_computation | loop fusion | flops 19200000 | bytes 48096000 | tf_op jit(solution)/shard_map/convert_element_type | solution.py:131
  394.6 13.2 %convert_element_type.107 = bf16[5,2,200,1536]{2,1,3,0:T(2,128)(2,1)} reshape(bf16[5,400,2,12,64]{1,4,3,2,0:T(8,128)(2,1)} %copy.73) | data formatting | bytes 12288000 | tf_op jit(solution)/shard_map/convert_element_type | solution.py:151
  407.7 19.6 %copy.74 = bf16[5,2,200,1536]{3,2,0,1:T(8,128)(2,1)} copy(bf16[5,2,200,1536]{2,1,3,0:T(2,128)(2,1)} %convert_element_type.107) | data formatting | bytes 12288000 | tf_op jit(solution)/shard_map/convert_element_type | solution.py:151
  427.4 11.2 %convolution_bitcast_fusion.1 = f32[1,768,3072]{2,1,0:T(8,128)} fusion(bf16[1000,3072]{1,0:T(8,128)(2,1)} %add_convert_fusion, f32[1000,768]{1,0:T(8,128)} %get-tuple-element.89, f32[768]{0:T(1024)S(1)} %reduce.5, f32[768]{0:T(1024)S(1)} %reduce.4, f32[1000]{0:T(1024)S(1)} %fusion.34, f32[1000]{0:T(1024)S(1)} %broadcast_multiply_fusion.1), kind=kOutput, calls=%fused_computation.32 | convolution fusion | flops 4722432000 | bytes 18667328 | tf_op jit(solution)/shard_map/dot_general | solution.py:25
  438.6 10.4 %convolution_bitcast_fusion = f32[1,3072,768]{2,1,0:T(8,128)} fusion(bf16[1000,3072]{1,0:T(8,128)(2,1)} %get-tuple-element.80, bf16[1000,768]{1,0:T(8,128)(2,1)S(1)} %copy-done.30), kind=kOutput, calls=%fused_computation.31 | convolution fusion | flops 4718592000 | bytes 17117184 | tf_op jit(solution)/shard_map/dot_general | solution.py:25
  449.2 11.3 %fusion.32 = bf16[5,200,12,64]{1,3,2,0:T(8,128)(2,1)} fusion(bf16[5,12,200,400]{3,2,1,0:T(8,128)(2,1)} %copy-done.1, bf16[5,400,2,12,64]{1,4,3,2,0:T(8,128)(2,1)} %reshape_reshape.3), kind=kOutput, calls=%fused_computation.75 | convolution fusion | flops 615936000 | bytes 17756160 | tf_op jit(solution)/shard_map/ghqk,gkhe->gqhe/dot_general | solution.py:133
  478.3 25.1 %reduce-scatter.2.cloned.1.call-done = bf16[5,1,200,1536]{3,2,0,1:T(8,128)(2,1)} async-done(((bf16[5,2,200,1536]{3,2,0,1:T(8,128)(2,1)}), bf16[5,1,200,1536]{3,2,0,1:T(8,128)(2,1)}) %reduce-scatter.2.cloned.1.call-update) | async-done | bytes 3072016 | tf_op jit(solution)/shard_map/reduce_scatter | solution.py:150
  517.7 36.7 %all-reduce.1 = (f32[1,768]{1,0:T(1,128)}, f32[1,768]{1,0:T(1,128)}) all-reduce(f32[1,768]{1,0:T(1,128)} %broadcast_in_dim.76, f32[1,768]{1,0:T(1,128)} %broadcast_in_dim.77), channel_id=1, replica_groups=mesh['dp'=16,'stream'=2] {'dp'}, use_global_device_ids=true, to_apply=%region_20.21 | all-reduce | flops 1536 | bytes 12288 | tf_op jit(solution)/shard_map/psum | solution.py:120
  569.6 38.9 %psum.49 = f32[4,768]{1,0:T(4,128)S(1)} all-reduce(f32[4,768]{1,0:T(4,128)} %pad_maximum_fusion.5), channel_id=1, replica_groups=mesh['dp'=16,'stream'=2] {'dp','stream'}, use_global_device_ids=true, to_apply=%region_16.17 | all-reduce | flops 3072 | bytes 24576 | tf_op jit(solution)/shard_map/psum | solution.py:160
  613.4 165.4 %all-reduce.8.cloned.1.call-done = (f32[1,768,3072]{2,1,0:T(8,128)}, f32[1,3072,768]{2,1,0:T(8,128)}) async-done(((f32[1,768,3072]{2,1,0:T(8,128)}, f32[1,3072,768]{2,1,0:T(8,128)}), (f32[1,768,3072]{2,1,0:T(8,128)}, f32[1,3072,768]{2,1,0:T(8,128)})) %all-reduce.8.cloned.1.call-update) | async-done | bytes 18874384 | tf_op jit(solution)/shard_map/psum | solution.py:120
  778.8 197.0 %all-reduce.6.cloned.1.call-done = (f32[768,2304]{1,0:T(8,128)}, f32[768,768]{1,0:T(8,128)}) async-done(((f32[768,2304]{1,0:T(8,128)}, f32[768,768]{1,0:T(8,128)}), (f32[768,2304]{1,0:T(8,128)}, f32[768,768]{1,0:T(8,128)})) %all-reduce.6.cloned.1.call-update) | async-done | bytes 9437200 | tf_op jit(solution)/shard_map/psum | solution.py:160
  (139 shorter events, 189.6 us)
Async XLA Ops:
  8.0 10.4 %copy-start = (bf16[768,2304]{1,0:T(8,128)(2,1)S(1)}, bf16[768,2304]{1,0:T(8,128)(2,1)}, u32[]{:S(2)}) copy-start(bf16[768,2304]{1,0:T(8,128)(2,1)} %param.17) | copy-start | bytes 10616836
  12.5 11.3 %copy-start.16 = (f32[1000]{0:T(1024)}, f32[1000]{0:T(1024)S(1)}, u32[]{:S(2)}) copy-start(f32[1000]{0:T(1024)S(1)} %div.47) | copy-start | bytes 12004
  63.7 76.1 %all-to-all-start = ((bf16[2,5,1,200,1536]{4,3,2,1,0:T(8,128)(2,1)}), bf16[2,5,1,200,1536]{4,3,2,1,0:T(8,128)(2,1)}, u32[]{:S(2)}, u32[]{:S(2)}) async-start(bf16[2,5,1,200,1536]{4,3,2,1,0:T(8,128)(2,1)} %copy.63), calls=%async_computation | async-start | bytes 12288000 | tf_op jit(solution)/shard_map/all_to_all | solution.py:65
  70.0 433.5 %reduce-scatter.2.cloned.1.call-start = ((), (), s32[]{:S(2)}) async-start(), calls=%async_computation.2 | async-start | bytes 9216000 | tf_op jit(solution)/shard_map/reduce_scatter | solution.py:150
  188.1 11.5 %copy-start.3 = (bf16[5,400,2,12,64]{1,4,3,2,0:T(8,128)(2,1)S(1)}, bf16[5,400,2,12,64]{1,4,3,2,0:T(8,128)(2,1)}, u32[]{:S(2)}) copy-start(bf16[5,400,2,12,64]{1,4,3,2,0:T(8,128)(2,1)} %reshape_reshape.3) | copy-start | bytes 18432004
  231.0 35.5 %copy-start.13 = (bf16[5,1,200,768]{3,2,1,0:T(8,128)(2,1)S(1)}, bf16[5,1,200,768]{3,2,1,0:T(8,128)(2,1)}, u32[]{:S(2)}) copy-start(bf16[5,1,200,768]{3,2,1,0:T(8,128)(2,1)} %fusion.25) | copy-start | bytes 4608004
  266.5 15.5 %copy-start.2 = (f32[1000,768]{1,0:T(8,128)S(1)}, f32[1000,768]{1,0:T(8,128)}, u32[]{:S(2)}) copy-start(f32[1000,768]{1,0:T(8,128)} %get-tuple-element.89) | copy-start | bytes 9216004
  282.0 10.3 %copy-start.9 = (bf16[5,1,200,768]{3,2,1,0:T(8,128)(2,1)S(1)}, bf16[5,1,200,768]{3,2,1,0:T(8,128)(2,1)}, u32[]{:S(2)}) copy-start(bf16[5,1,200,768]{3,2,1,0:T(8,128)(2,1)} %param.25) | copy-start | bytes 4608004
  282.0 10.3 %copy-start.27 = (f32[768]{0:T(1024)S(1)}, f32[768]{0:T(1024)}, u32[]{:S(2)}) copy-start(f32[768]{0:T(1024)} %param.20) | copy-start | bytes 9220
  282.0 10.3 %copy-start.29 = (bf16[1000,3072]{1,0:T(8,128)(2,1)S(1)}, bf16[1000,3072]{1,0:T(8,128)(2,1)}, u32[]{:S(2)}) copy-start(bf16[1000,3072]{1,0:T(8,128)(2,1)} %get-tuple-element.80) | copy-start | bytes 18432004
  292.3 10.7 %copy-start.5 = (f32[1000,768]{1,0:T(8,128)S(1)}, f32[1000,768]{1,0:T(8,128)}, u32[]{:S(2)}) copy-start(f32[1000,768]{1,0:T(8,128)} %get-tuple-element.90) | copy-start | bytes 9216004
  320.3 22.1 %copy-start.6 = (bf16[5,200,12,64]{1,3,2,0:T(8,128)(2,1)S(1)}, bf16[5,200,12,64]{1,3,2,0:T(8,128)(2,1)}, u32[]{:S(2)}) copy-start(bf16[5,200,12,64]{1,3,2,0:T(8,128)(2,1)} %copy.70) | copy-start | bytes 4608004
  320.3 22.1 %copy-start.11 = (f32[5,12,200]{2,1,0:T(8,128)S(1)}, f32[5,12,200]{2,1,0:T(8,128)}, u32[]{:S(2)}) copy-start(f32[5,12,200]{2,1,0:T(8,128)} %log_add_fusion) | copy-start | bytes 144004
  355.0 20.8 %copy-start.7 = (bf16[5,200,1,12,64]{1,0,4,3,2:T(8,128)(2,1)S(1)}, bf16[5,200,1,12,64]{1,0,4,3,2:T(8,128)(2,1)}, u32[]{:S(2)}) copy-start(bf16[5,200,1,12,64]{1,0,4,3,2:T(8,128)(2,1)} %slice.34) | copy-start | bytes 4608004
  427.3 351.5 %all-reduce.8.cloned.1.call-start = ((), (), s32[]{:S(2)}) async-start(), calls=%async_computation.4 | async-start | bytes 37748736 | tf_op jit(solution)/shard_map/psum | solution.py:120
  427.4 11.2 %copy-start.30 = (bf16[1000,768]{1,0:T(8,128)(2,1)S(1)}, bf16[1000,768]{1,0:T(8,128)(2,1)}, u32[]{:S(2)}) copy-start(bf16[1000,768]{1,0:T(8,128)(2,1)} %get-tuple-element.86) | copy-start | bytes 4608004
  449.0 526.9 %all-reduce.6.cloned.1.call-start = ((), (), s32[]{:S(2)}) async-start(), calls=%async_computation.3 | async-start | bytes 18874368 | tf_op jit(solution)/shard_map/psum | solution.py:160
  460.6 12.6 %copy-start.24 = (f32[768]{0:T(1024)S(1)}, f32[768]{0:T(1024)}, u32[]{:S(2)}) copy-start(f32[768]{0:T(1024)} %param.19) | copy-start | bytes 9220
  513.2 41.2 %copy-start.17 = (f32[1000]{0:T(1024)S(1)}, f32[1000]{0:T(1024)}, u32[]{:S(2)}) copy-start(f32[1000]{0:T(1024)} %copy-done.16) | copy-start | bytes 12004
  513.3 41.2 %copy-start.19 = (f32[1000]{0:T(1024)S(1)}, f32[1000]{0:T(1024)}, u32[]{:S(2)}) copy-start(f32[1000]{0:T(1024)} %copy-done.18) | copy-start | bytes 12004
  513.3 41.2 %copy-start.25 = (f32[768]{0:T(1024)S(1)}, f32[768]{0:T(1024)}, u32[]{:S(2)}) copy-start(f32[768]{0:T(1024)} %param.15) | copy-start | bytes 9220
  982.5 10.7 %slice-start.1 = ((s8[9437184]{0:T(1024)(128)(4,1)}), s8[4194304]{0:T(1024)(128)(4,1)S(1)}, s32[]{:S(2)}) async-start(s8[9437184]{0:T(1024)(128)(4,1)} %bitcast.115), calls=%async_computation.6 | async-start | bytes 8388608
  983.9 9.3 slice-start.2
  983.9 9.3 slice-start.3
  (15 other events, 69.9 us)
Sparse Core Ops, SparseCore 0:
  427.4 75.9 reduce-scatter.1
Sparse Core Ops, SparseCore 1:
  449.1 329.7 all-reduce.7
  785.2 190.6 all-reduce.5
